TPU v7x, 128 devices: a whole 4x4x4 slice. The times are simulated.
128 devices in a mesh: expert: 16 (over z, x), replica: 8 (over y, core).
Axes of the slice: x: 4, y: 4, z: 4, core: 2. Of those that a mesh axis runs over, the one named last changes fastest.
Arguments:
- mantissa: bfloat16 [4194304, 128], P(('expert', 'replica')), may hold values from -4 to 4
- scales: bfloat16 [4194304], P(('expert', 'replica')), may hold values from 0.25 to 4
- counts: int32 [8192], P(('expert', 'replica')), may hold values from 256 to 512, as said below
- owner_map: int32 [1024], replicated, may hold values from 0 to 1023, each once
Outputs:
- out_mantissa: bfloat16 [32768, 128], P(('expert', 'replica'))
- out_scales: float32 [32768], P(('expert', 'replica'))
Inputs may be any that keep to these rules, and one draw needn't show every extreme that they name: A device's live blocks of an expert are that expert's first counts blocks; some expert has 512 live blocks on every device, and some expert has its last block dead on every device. `owner_map`: each of 0 to 1023 appears once.
All inputs are finite; a program needn't handle non-finite values. Where the computation divides by a largest or mean magnitude, that divisor is 1e-20 or more.
Results may differ from a plain program's by a relative error of at most 0.001.
Values may be sent and summed in bfloat16 or wider, within the bound.
A program may use at most 128 MiB of HBM per device.

v0:
```python
import jax
import jax.numpy as jnp
from jax import lax
from jax.sharding import Mesh
from jax.sharding import PartitionSpec as P

GROUP = 32
EXPERT = ("expert_0", "expert_1")
REPLICA = ("replica_0", "replica_1")
EXPERT_REPLICA = ("expert_0", "expert_1", "replica_0", "replica_1")


clip_target = 0.05
epsilon = 1e-06


def laid_out(tiles, dim):
    tiles = jnp.moveaxis(tiles, 0, dim)
    dims = tiles.shape
    return tiles.reshape(*dims[:dim], dims[dim] * dims[dim + 1], *dims[dim + 2 :])


def gather_in_order(shard, axes, sequence):
    tiles = shard
    for k in sequence:
        tiles = lax.all_gather(tiles, axes[k])
    done = sequence[::-1]
    back = [done.index(k) for k in range(len(axes))]
    tiles = tiles.transpose(*back, *range(len(axes), tiles.ndim))
    return tiles.reshape(-1, *shard.shape)


def gather_axes(shard, axes, sequence, dim):
    return laid_out(gather_in_order(shard, axes, sequence), dim)


def grouped_exchange(shard, axis, split_dim, concat_dim, work, item_dim, out_dim):
    items = jax.tree.leaves(shard)[0].shape[item_dim]
    count = 2 if items % 2 == 0 else 1
    gathered = []
    for k in range(count):
        group = jax.tree.map(
            lambda a: lax.slice_in_dim(
                a, k * (items // count), (k + 1) * (items // count), axis=item_dim
            ),
            shard,
        )
        gathered.append(
            work(
                lax.all_to_all(
                    group, axis, split_axis=split_dim, concat_axis=concat_dim, tiled=True
                )
            )
        )
    return jax.tree.map(lambda *parts: jnp.concatenate(parts, axis=out_dim), *gathered)


def one_axis_at_a_time(shard, axes):
    for axis in axes:
        shard = lax.psum(shard, axis)
    return shard


def sum_sources(received):
    values, weights = received
    return jnp.sum(values.astype(jnp.float32) * weights.astype(jnp.float32)[:, :, None], axis=0)


def by_groups(array, group_ids):
    shape = array.shape
    grouped = array.reshape((shape[0] // GROUP, GROUP) + shape[1:])
    picked = jnp.take(grouped, group_ids, axis=0)
    return picked.reshape((group_ids.shape[0] * GROUP,) + shape[1:])


def local(mantissa, scales, counts, owner_map):
    block_total = mantissa.shape[0]
    expert_count = counts.shape[0]
    per_expert = block_total // expert_count
    block_width = mantissa.shape[1]
    n_expert = lax.axis_size(EXPERT)
    n_replica = lax.axis_size(REPLICA)
    sources = n_expert * n_replica
    owned_rows = block_total // sources
    count_table = gather_axes(counts, EXPERT_REPLICA, (0, 1, 2, 3), 0).reshape(
        sources, expert_count
    )
    position = jnp.arange(per_expert, dtype=jnp.int32)
    is_live = (counts[:, None] > position[None, :]).reshape(block_total)
    live_scale = jnp.where(is_live, scales, jnp.zeros_like(scales))
    ordered_values = by_groups(mantissa, owner_map).reshape(sources, owned_rows, block_width)
    ordered_scales = by_groups(live_scale, owner_map).reshape(sources, owned_rows)
    summed = grouped_exchange(
        (ordered_values, ordered_scales), EXPERT_REPLICA, 0, 0, sum_sources, 1, 0
    )
    my_groups = lax.dynamic_slice_in_dim(
        owner_map, lax.axis_index(EXPERT_REPLICA) * (owned_rows // GROUP), owned_rows // GROUP
    )
    my_blocks = (my_groups[:, None] * GROUP + jnp.arange(GROUP, dtype=jnp.int32)[None, :]).reshape(
        owned_rows
    )
    expert_loads = jnp.take(count_table, my_blocks // per_expert, axis=1)
    contributors = jnp.sum(
        (expert_loads > (my_blocks % per_expert)[None, :]).astype(jnp.int32), axis=0
    )
    averaged = summed / jnp.maximum(contributors, 1).astype(jnp.float32)[:, None]
    square_total = one_axis_at_a_time(jnp.sum(averaged * averaged), EXPERT_REPLICA)
    root_mean = jnp.sqrt(square_total / (block_total * block_width) + epsilon)
    clip_factor = jnp.minimum(1.0, clip_target / root_mean)
    clipped = averaged * clip_factor
    block_peak = jnp.max(jnp.abs(clipped), axis=1) + epsilon
    return ((clipped / block_peak[:, None]).astype(jnp.bfloat16), block_peak)


def solution(mesh):
    split = Mesh(
        mesh.devices.reshape(4, 4, 4, 2), ("expert_0", "expert_1", "replica_0", "replica_1")
    )
    placed = (P(EXPERT_REPLICA, None), P(EXPERT_REPLICA), P(EXPERT_REPLICA), P())
    return jax.shard_map(
        local,
        mesh=split,
        in_specs=placed,
        out_specs=(P(EXPERT_REPLICA, None), P(EXPERT_REPLICA)),
        check_vma=False,
    )
```

profile of v0, /device:TPU:0, one launch (start us, length us, event | category | flops | bytes accessed | tf_op | source)
XLA Modules:
  0.0 245.0 jit_solution(12483623225715167248)
XLA Ops:
  0.6 0.7 fusion.1
  1.3 0.7 compare_and_fusion
  2.0 0.1 broadcast_in_dim.48
  2.1 0.1 copy.21
  2.2 0.8 fusion
  3.0 0.9 broadcast_select_fusion
  3.8 0.2 reshape.160
  4.0 3.2 %gather_fusion.1 = bf16[1024,32]{1,0:T(8,128)(2,1)S(1)} fusion(bf16[1024,32]{1,0:T(8,128)(2,1)S(1)} %reshape.160, s32[1024]{0:T(1024)S(1)} %fusion.1), kind=kCustom, calls=%fused_computation.1 | custom fusion | bytes 135168 | tf_op jit(solution)/shard_map/jit(_take)/gather | solution.py:72
  7.2 0.2 gather.19
  7.4 0.1 copy.23
  7.6 0.8 copy.25
  8.3 11.2 %all-to-all-start.3 = ((bf16[128,1,128]{2,1,0:T(2,128)(2,1)}), bf16[128,1,128]{2,1,0:T(2,128)(2,1)S(1)}, u32[]{:S(2)}, u32[]{:S(2)}) async-start(bf16[128,1,128]{2,1,0:T(2,128)(2,1)} %copy.25), calls=%async_computation.3 | async-start | bytes 131072 | tf_op jit(solution)/shard_map/all_to_all | solution.py:50
  19.5 13.3 %gather_fusion = bf16[1024,32,128]{2,1,0:T(8,128)(2,1)} fusion(bf16[1024,32,128]{2,1,0:T(8,128)(2,1)} %bitcast.23, s32[1024]{0:T(1024)S(1)} %fusion.1), kind=kCustom, calls=%fused_computation | custom fusion | bytes 16781312 | tf_op jit(solution)/shard_map/jit(_take)/gather | solution.py:72
  32.8 0.1 copy.22
  32.9 7.6 %bitcast_select_fusion = bf16[128,256,128]{2,1,0:T(8,128)(2,1)} fusion(pred[128,256]{1,0:T(8,128)(4,1)S(1)} %copy.22, bf16[128,256,128]{2,1,0:T(8,128)(2,1)} %bitcast.22), kind=kLoop, calls=%fused_computation.3 | loop fusion | flops 4194304 | bytes 16809984 | tf_op jit(solution)/shard_map/jit(_take)/select_n | solution.py:72
  40.6 0.7 copy.24
  41.3 0.0 all-to-all-done.3
  41.3 9.8 %all-to-all-start.1 = ((bf16[128,1,128]{2,1,0:T(2,128)(2,1)}), bf16[128,1,128]{2,1,0:T(2,128)(2,1)S(1)}, u32[]{:S(2)}, u32[]{:S(2)}) async-start(bf16[128,1,128]{2,1,0:T(2,128)(2,1)} %copy.24), calls=%async_computation.1 | async-start | bytes 131072 | tf_op jit(solution)/shard_map/all_to_all | solution.py:50
  51.1 6.1 %fusion.2 = (bf16[128,128,128]{2,1,0:T(8,128)(2,1)}, bf16[128,128,128]{2,1,0:T(8,128)(2,1)}) fusion(bf16[128,256,128]{2,1,0:T(8,128)(2,1)} %bitcast_select_fusion), kind=kLoop, calls=%fused_computation.40 | loop fusion | bytes 16777216 | tf_op jit(solution)/shard_map/slice | solution.py:43
  57.1 3.3 %all-to-all-done.1 = bf16[128,1,128]{2,1,0:T(2,128)(2,1)S(1)} async-done(((bf16[128,1,128]{2,1,0:T(2,128)(2,1)}), bf16[128,1,128]{2,1,0:T(2,128)(2,1)S(1)}, u32[]{:S(2)}, u32[]{:S(2)}) %all-to-all-start.1) | async-done | bytes 32800 | tf_op jit(solution)/shard_map/all_to_all | solution.py:50
  60.4 0.0 copy-start.2
  60.4 0.0 copy-start.1
  60.4 59.5 %all_to_all.28 = bf16[128,128,128]{2,1,0:T(8,128)(2,1)} all-to-all(bf16[128,128,128]{2,1,0:T(8,128)(2,1)} %get-tuple-element.5), channel_id=1, replica_groups=mesh['expert_0'=4,'expert_1'=4,'replica_0'=4,'replica_1'=2] {'expert_0',..., dimensions={0} | all-to-all | bytes 8388608 | tf_op jit(solution)/shard_map/all_to_all | solution.py:50
  120.0 5.8 %all-to-all-start = ((bf16[128,128,128]{2,1,0:T(8,128)(2,1)}), bf16[128,128,128]{2,1,0:T(8,128)(2,1)}, u32[]{:S(2)}, u32[]{:S(2)}) async-start(bf16[128,128,128]{2,1,0:T(8,128)(2,1)} %get-tuple-element.4), calls=%async_computation | async-start | bytes 8388608 | tf_op jit(solution)/shard_map/all_to_all | solution.py:50
  125.8 0.8 dynamic-slice_multiply_fusion
  126.6 0.1 iota_add_fusion
  126.7 0.1 add.131
  126.7 0.1 add.128
  126.8 0.0 copy-done.2
  126.8 0.6 dynamic-slice
  128.1 0.0 copy-done.1
  128.1 0.2 dynamic-update-slice
  128.3 22.1 %all-reduce = s32[256]{0:T(256)S(1)} all-reduce(s32[256]{0:T(256)S(1)} %dynamic-update-slice), channel_id=2, replica_groups=mesh['expert_0'=4,'expert_1'=4,'replica_0'=4,'replica_1'=2] {'expert_0'}, use_global_device_ids=true, to_apply=%add | all-reduce | flops 256 | bytes 2048
  150.4 0.1 reshape.196
  150.5 27.1 %all-gather.4 = s32[4,4,64]{2,1,0:T(4,128)S(1)} all-gather(s32[1,4,64]{2,1,0:T(4,128)S(1)} %reshape.196), channel_id=3, replica_groups=mesh['expert_0'=4,'expert_1'=4,'replica_0'=4,'replica_1'=2] {'expert_1'}, dimensions={0}, use_global_device_ids=true | all-gather | bytes 5120 | tf_op jit(solution)/shard_map/all_gather | solution.py:26
  177.6 22.5 %all-gather.2 = s32[16,4,64]{2,1,0:T(4,128)S(1)} all-gather(s32[4,4,64]{2,1,0:T(4,128)S(1)} %all-gather.4), channel_id=4, replica_groups=mesh['expert_0'=4,'expert_1'=4,'replica_0'=4,'replica_1'=2] {'replica_0'}, dimensions={0}, use_global_device_ids=true | all-gather | bytes 20480 | tf_op jit(solution)/shard_map/all_gather | solution.py:26
  200.1 1.8 all-gather.3
  202.0 0.1 copy.29
  202.1 0.7 gather_fusion.2
  202.9 0.2 convert_reduce_fusion
  203.1 0.1 convert_element_type.49
  203.2 0.1 convert_element_type.48
  203.2 4.4 %multiply_reduce_fusion = f32[128,128]{1,0:T(8,128)S(1)} fusion(bf16[128,128,128]{2,1,0:T(8,128)(2,1)} %all_to_all.28, f32[128,128]{1,0:T(8,128)S(1)} %bitcast.25), kind=kLoop, calls=%fused_computation.4 | loop fusion | flops 6275072 | bytes 4325376 | tf_op jit(solution)/shard_map/reduce_sum | solution.py:66
  207.6 0.0 all-to-all-done
  207.7 4.4 %multiply_reduce_fusion.1 = f32[128,128]{1,0:T(8,128)S(1)} fusion(bf16[128,128,128]{2,1,0:T(8,128)(2,1)} %all-to-all-done, f32[128,128]{1,0:T(8,128)S(1)} %bitcast.24), kind=kLoop, calls=%fused_computation.5 | loop fusion | flops 6275072 | bytes 4325376 | tf_op jit(solution)/shard_map/reduce_sum | solution.py:66
  212.0 0.7 multiply_reduce_fusion.2
  212.8 8.3 %psum.28 = f32[]{:T(128)} all-reduce(f32[]{:T(128)} %get-tuple-element.2), channel_id=1, replica_groups=mesh['expert_0'=4,'expert_1'=4,'replica_0'=4,'replica_1'=2] {'expert_0'}, use_global_device_ids=true, to_apply=%region_4.5 | all-reduce | flops 1 | bytes 8 | tf_op jit(solution)/shard_map/psum | solution.py:60
  221.1 8.3 %psum.29 = f32[]{:T(128)} all-reduce(f32[]{:T(128)} %psum.28), channel_id=1, replica_groups=mesh['expert_0'=4,'expert_1'=4,'replica_0'=4,'replica_1'=2] {'expert_1'}, use_global_device_ids=true, to_apply=%region_5.6 | all-reduce | flops 1 | bytes 8 | tf_op jit(solution)/shard_map/psum | solution.py:60
  229.4 10.9 %psum.30 = f32[]{:T(128)} all-reduce(f32[]{:T(128)} %psum.29), channel_id=1, replica_groups=mesh['expert_0'=4,'expert_1'=4,'replica_0'=4,'replica_1'=2] {'replica_0'}, use_global_device_ids=true, to_apply=%region_6.7 | all-reduce | flops 1 | bytes 8 | tf_op jit(solution)/shard_map/psum | solution.py:60
  240.3 3.1 %psum.31 = f32[]{:T(128)} all-reduce(f32[]{:T(128)} %psum.30), channel_id=1, replica_groups=mesh['expert_0'=4,'expert_1'=4,'replica_0'=4,'replica_1'=2] {'replica_1'}, use_global_device_ids=true, to_apply=%region_7.8 | all-reduce | flops 1 | bytes 8 | tf_op jit(solution)/shard_map/psum | solution.py:60
  244.1 0.1 abs_reduce_fusion
  244.2 0.0 copy-start
  244.2 0.7 divide_convert_fusion
  244.9 0.0 copy-done
  (14 shorter events, 0.2 us)
Async XLA Ops:
  8.3 33.0 %all-to-all-start.3 = ((bf16[128,1,128]{2,1,0:T(2,128)(2,1)}), bf16[128,1,128]{2,1,0:T(2,128)(2,1)S(1)}, u32[]{:S(2)}, u32[]{:S(2)}) async-start(bf16[128,1,128]{2,1,0:T(2,128)(2,1)} %copy.25), calls=%async_computation.3 | async-start | bytes 131072 | tf_op jit(solution)/shard_map/all_to_all | solution.py:50
  41.3 19.1 %all-to-all-start.1 = ((bf16[128,1,128]{2,1,0:T(2,128)(2,1)}), bf16[128,1,128]{2,1,0:T(2,128)(2,1)S(1)}, u32[]{:S(2)}, u32[]{:S(2)}) async-start(bf16[128,1,128]{2,1,0:T(2,128)(2,1)} %copy.24), calls=%async_computation.1 | async-start | bytes 131072 | tf_op jit(solution)/shard_map/all_to_all | solution.py:50
  60.4 66.4 %copy-start.2 = (u32[128]{0:T(128)S(1)}, u32[128]{0:T(128)}, u32[]{:S(2)}) copy-start(u32[128]{0:T(128)} %constant.114) | copy-start | bytes 1540
  60.4 67.6 %copy-start.1 = (s32[64]{0:T(128)S(1)}, s32[64]{0:T(128)}, u32[]{:S(2)}) copy-start(s32[64]{0:T(128)} %param.6) | copy-start | bytes 772
  120.0 87.7 %all-to-all-start = ((bf16[128,128,128]{2,1,0:T(8,128)(2,1)}), bf16[128,128,128]{2,1,0:T(8,128)(2,1)}, u32[]{:S(2)}, u32[]{:S(2)}) async-start(bf16[128,128,128]{2,1,0:T(8,128)(2,1)} %get-tuple-element.4), calls=%async_computation | async-start | bytes 8388608 | tf_op jit(solution)/shard_map/all_to_all | solution.py:50
  244.2 0.8 copy-start
where the time goes:
time: 247 us; the launch traced here: 245 us
  blocking collectives  164 us (66%)
  local copies, waits for them, and re-layouts  26.8 us (11%)
  starting transfers between devices  26.8 us (11%)
  other arithmetic  22.2 us (9%)
  waiting for transfers between devices  3.29 us (1%)
    all_to_all x1, blocking collectives, grouped_exchange(): lax.all_to_all(group, axis, split_axis=split_dim, concat_axis=concat_dim,...  59.5 us
    all_gather x3, blocking collectives, gather_in_order(): tiles = lax.all_gather(tiles, axes[k])  51.4 us
    psum x4, blocking collectives, one_axis_at_a_time(): shard = lax.psum(shard, axis)  30.6 us
    all_to_all x3, starting transfers between devices, grouped_exchange(): lax.all_to_all(group, axis, split_axis=split_dim, concat_axis=concat_dim,...  26.8 us
    unnamed x1, blocking collectives  22.1 us
    gather x4, local copies, waits for them, and re-layouts, by_groups(): picked = jnp.take(grouped, group_ids, axis=0)  16.8 us
    reduce_sum x2, other arithmetic, sum_sources(): jnp.sum(values.astype(jnp.float32) * weights.astype(jnp.float32)[:, :, No...  8.77 us
    select_n x2, other arithmetic, by_groups(): picked = jnp.take(grouped, group_ids, axis=0)  7.65 us
  transfers between devices with their start and end apart: 3, of which 1 were waited for; matrix products, arithmetic and copies ran while one was open for 14% of the time, Pallas kernels for 0%

commit v1 on v0

v1 whole, which is shorter than its diff:
```python
import jax
import jax.numpy as jnp
from jax import lax
from jax.experimental import pallas as pl
from jax.experimental.pallas import tpu as pltpu
from jax.sharding import PartitionSpec as P

MESH = pl.DeviceIdType.MESH
AXES = ("expert", "replica")
GROUP = 32
CLIP = 0.05
EPS = 1e-06
ROWS = (96, 80, 80)
START = (0, 96, 176)
PIECES = (
    ((0, 0, 32), (1, 0, 32), (2, 0, 32)),
    ((3, 0, 32), (4, 0, 32), (5, 0, 16)),
    ((5, 16, 16), (6, 0, 32), (7, 0, 32)),
)
ORDER = (2, 1, 3, 0)
FAR, OWN, BOTH = 0, 1, 2
TOP = 32767.0
LOADS = 8


def pick(k, a, b, c):
    return a * ((1 - k) * (2 - k) // 2) + b * (k * (2 - k)) + c * (k * (k - 1) // 2)


def kernel(owner, mant_hbm, scale, eye, out, peak, mant, far_scale, fin, red_send, red_recv, *rest):
    rest = list(rest)

    def take(n):
        head = rest[:n]
        del rest[:n]
        return head

    dsend, drecv, own, near = take(3), take(3), take(3), take(3)
    own_n, near_n = take(3), take(3)
    q1, r1, t1, u1 = take(3), take(3), take(3), take(3)
    mid, mid_n = take(3), take(3)
    q2, r2, t2, u2 = take(3), take(3), take(3), take(3)
    q3, r3, t3, u3 = take(3), take(3), take(3), take(3)
    load_sem, pair_sem, fs_sem, sem1, sem2, sem3, red_sem = rest

    e, r = lax.axis_index("expert"), lax.axis_index("replica")
    z, x = lax.div(e, 4), lax.rem(e, 4)
    y, core = lax.div(r, 2), lax.rem(r, 2)
    partner = (e, z * 0 + y * 2 + 1 - core)

    def moved(c, p, ra, rb, rc):
        first = lax.rem(p + c, 3)
        dx, dy, dz = (pick(lax.rem(dim + 3 - first, 3), ra, rb, rc) for dim in range(3))
        return lax.rem(x + dx, 4), lax.rem(y + dy, 4), lax.rem(z + dz, 4)

    def chip_of(c, p, ra, rb, rc):
        x2, y2, z2 = moved(c, p, ra, rb, rc)
        return (z2 * 4 + x2) * 4 + y2

    def peer(p, role, rel):
        rels = [0, 0, 0]
        rels[role] = rel
        x2, y2, z2 = moved(core, p, *rels)
        return (z2 * 4 + x2, y2 * 2 + core)

    def remote(src, dst, sems, device):
        return pltpu.make_async_remote_copy(
            src_ref=src, dst_ref=dst, send_sem=sems.at[0], recv_sem=sems.at[1],
            device_id=device, device_id_type=MESH,
        )

    def load(i):
        part = pl.ds(i * (1024 // LOADS), 1024 // LOADS)
        return pltpu.make_async_copy(mant_hbm.at[part], mant.at[part], load_sem.at[i])

    for i in range(LOADS):
        load(i).start()

    barrier = pltpu.get_barrier_semaphore()
    greeted = [partner]
    for rel in (1, 2, 3):
        greeted += [(z * 4 + lax.rem(x + rel, 4), r), (e, lax.rem(y + rel, 4) * 2 + core),
                    (lax.rem(z + rel, 4) * 4 + x, r)]
    for device in greeted:
        pl.semaphore_signal(barrier, inc=1, device_id=device, device_id_type=MESH)
    pl.semaphore_wait(barrier, len(greeted))

    fs_copy = remote(scale.at[1 - core], far_scale, fs_sem, partner)
    fs_copy.start()
    for i in range(LOADS):
        load(i).wait()

    def pair_copy(p, k):
        return remote(dsend[p].at[k], drecv[p].at[k], pair_sem.at[p, k], partner)

    for k in range(4):
        for p in range(3):

            @pl.loop(0, 4)
            def _(rb, p=p, k=k):
                for rc in range(4):
                    chip = chip_of(1 - core, p, ORDER[k], rb, rc)
                    first = (chip * 2 + 1 - core) * 8
                    at = 0
                    for g, r0, n in PIECES[p]:
                        dsend[p][k, rb * 4 + rc, pl.ds(at, n)] = mant[owner[first + g], pl.ds(r0, n)]
                        at += n

            pair_copy(p, k).start()

    def column(row, n):
        return jnp.sum(row * eye[pl.ds(0, n)], axis=1, keepdims=True)

    def product(p, k, rel, rb, rc):
        n = ROWS[p]
        chip = chip_of(core, p, rel, rb, rc)
        first = (chip * 2 + core) * 8
        mine = jnp.concatenate(
            [mant[owner[first + g], pl.ds(r0, m)].astype(jnp.float32) for g, r0, m in PIECES[p]], axis=0
        )
        other = drecv[p][k, rb * 4 + rc].astype(jnp.float32)
        s1 = scale[core, p, pl.ds(chip, 1)]
        s2 = far_scale[p, pl.ds(chip, 1)]
        count = jnp.where(s1 > 0.0, 1.0, 0.0) + jnp.where(s2 > 0.0, 1.0, 0.0)
        return mine * column(s1, n) + other * column(s2, n), count

    def quantize(v):
        n = v.shape[0]
        most = jnp.maximum(jnp.max(jnp.abs(v), axis=1, keepdims=True), 1e-30)
        q = lax.round(v * (TOP / most), lax.RoundingMethod.TO_NEAREST_EVEN)
        step = jnp.sum((most * (1.0 / TOP)) * eye[pl.ds(0, n)], axis=0, keepdims=True)
        return q.astype(jnp.int32).astype(jnp.int16), step

    def restored(q, row):
        return q.astype(jnp.int32).astype(jnp.float32) * column(row, q.shape[0])

    def copies1(p, d, kind):
        device = peer(p, 0, 1 + 2 * d)
        return (
            remote(q1[p].at[d, kind], r1[p].at[d, kind], sem1.at[p, d, kind, 0], device),
            remote(t1[p].at[d, kind], u1[p].at[d, kind], sem1.at[p, d, kind, 1], device),
        )

    def send1(p, d, kind, values):
        coded = [quantize(v) for v, _ in values]
        for u, ((q, step), (_, count)) in enumerate(zip(coded, values)):
            q1[p][d, kind, u] = q
            t1[p][d, kind, 0, pl.ds(u, 1)] = step
            t1[p][d, kind, 1, pl.ds(u, 1)] = count
        for copy in copies1(p, d, kind):
            copy.start()

    fs_copy.wait_recv()
    for p in range(3):
        pair_copy(p, 0).wait_recv()

        @pl.loop(0, 2)
        def _(d, p=p):
            send1(p, d, FAR, [product(p, 0, 2, d * 2 + u // 4, u % 4) for u in range(8)])

    for p in range(3):
        for d in range(2):
            pair_copy(p, 1 + d).wait_recv()

        @pl.loop(0, 2)
        def _(d, p=p):
            send1(p, d, OWN, [product(p, 1 + d, 1 + 2 * d, (1 - d) * 2 + u // 4, u % 4) for u in range(8)])

    for p in range(3):

        @pl.loop(0, 2)
        def _(d, p=p):
            values = [product(p, 1 + d, 1 + 2 * d, d * 2 + u // 4, u % 4) for u in range(8)]
            for u, (v, count) in enumerate(values):
                near[p][d, u] = v
                near_n[p][d, pl.ds(u, 1)] = count

    for p in range(3):

        @pl.loop(0, 2)
        def _(d, p=p):
            for copy in copies1(p, d, FAR):
                copy.wait_recv()
            values = []
            for u in range(8):
                v = near[p][d, u] + restored(r1[p][d, FAR, u], u1[p][d, FAR, 0, pl.ds(u, 1)])
                values.append((v, near_n[p][d, pl.ds(u, 1)] + u1[p][d, FAR, 1, pl.ds(u, 1)]))
            send1(p, d, BOTH, values)

    for p in range(3):
        pair_copy(p, 3).wait_recv()

        @pl.loop(0, 2)
        def _(h, p=p):
            values = [product(p, 3, 0, h * 2 + u // 4, u % 4) for u in range(8)]
            for u, (v, count) in enumerate(values):
                own[p][h, u] = v
                own_n[p][h, pl.ds(u, 1)] = count

    def copies2(p, k):
        device = peer(p, 1, k)
        return (
            remote(q2[p].at[k - 1], r2[p].at[k - 1], sem2.at[p, k - 1, 0], device),
            remote(t2[p].at[k - 1], u2[p].at[k - 1], sem2.at[p, k - 1, 1], device),
        )

    def copies3(p, k):
        device = peer(p, 2, k)
        return (
            remote(q3[p].at[k - 1], r3[p].at[k - 1], sem3.at[p, k - 1, 0], device),
            remote(t3[p].at[k - 1], u3[p].at[k - 1], sem3.at[p, k - 1, 1], device),
        )

    for p in range(3):
        for d in range(2):
            for kind in (OWN, BOTH):
                for copy in copies1(p, d, kind):
                    copy.wait_recv()
        for rb in ORDER:
            h, values = rb // 2, []
            for rc in range(4):
                u = rb % 2 * 4 + rc
                v, count = own[p][h, u], own_n[p][h, pl.ds(u, 1)]
                for d, kind in ((h, BOTH), (1 - h, OWN)):
                    v = v + restored(r1[p][d, kind, u], u1[p][d, kind, 0, pl.ds(u, 1)])
                    count = count + u1[p][d, kind, 1, pl.ds(u, 1)]
                values.append((v, count))
            if rb:
                for rc, (v, count) in enumerate(values):
                    q2[p][rb - 1, rc], step = quantize(v)
                    t2[p][rb - 1, 0, pl.ds(rc, 1)] = step
                    t2[p][rb - 1, 1, pl.ds(rc, 1)] = count
                for copy in copies2(p, rb):
                    copy.start()
            else:
                for rc, (v, count) in enumerate(values):
                    mid[p][rc] = v
                    mid_n[p][pl.ds(rc, 1)] = count

    last = []
    for p in range(3):
        for k in (1, 3, 2):
            for copy in copies2(p, k):
                copy.wait_recv()
        values = []
        for rc in range(4):
            v, count = mid[p][rc], mid_n[p][pl.ds(rc, 1)]
            for k in range(3):
                v = v + restored(r2[p][k, rc], u2[p][k, 0, pl.ds(rc, 1)])
                count = count + u2[p][k, 1, pl.ds(rc, 1)]
            values.append((v, count))
        for rc in (2, 1, 3):
            v, count = values[rc]
            q3[p][rc - 1], step = quantize(v)
            t3[p][rc - 1, pl.ds(0, 1)] = step
            t3[p][rc - 1, pl.ds(1, 1)] = count
            for copy in copies3(p, rc):
                copy.start()
        mid[p][0] = values[0][0]
        mid_n[p][pl.ds(0, 1)] = values[0][1]

    square = jnp.zeros((8, 128), jnp.float32)
    for p in range(3):
        n = ROWS[p]
        for k in (1, 3, 2):
            for copy in copies3(p, k):
                copy.wait_recv()
        v, count = mid[p][0], mid_n[p][pl.ds(0, 1)]
        for k in range(3):
            v = v + restored(r3[p][k], u3[p][k, pl.ds(0, 1)])
            count = count + u3[p][k, pl.ds(1, 1)]
        mean = v / column(jnp.maximum(count, 1.0), n)
        fin[pl.ds(START[p], n)] = mean
        square = square + jnp.sum((mean * mean).reshape(n // 8, 8, 128), axis=0)
    total = jnp.sum(jnp.sum(square, axis=0, keepdims=True), axis=1, keepdims=True)

    levels = [[partner]] + [greeted[1 + dim :: 3] for dim in range(3)]
    reduce_copies = []
    for level, devices in enumerate(levels):
        red_send[level] = jnp.broadcast_to(total, (8, 128))
        copies = [
            remote(red_send.at[level], red_recv.at[level, k], red_sem.at[level, k], device)
            for k, device in enumerate(devices)
        ]
        for copy in copies:
            copy.start()
        for k, copy in enumerate(copies):
            copy.wait_recv()
            total = total + red_recv[level, k, pl.ds(0, 1), pl.ds(0, 1)]
        reduce_copies += copies

    root = jnp.sqrt(total / (32768 * 128) + EPS)
    factor = jnp.minimum(1.0, CLIP / root)
    for h in range(2):
        clipped = fin[pl.ds(h * 128, 128)] * factor
        top = jnp.max(jnp.abs(clipped), axis=1, keepdims=True) + EPS
        out[pl.ds(h * 128, 128)] = (clipped / top).astype(jnp.bfloat16)
        peak[pl.ds(h, 1)] = jnp.sum(top * eye[...], axis=0, keepdims=True)

    fs_copy.wait_send()
    for p in range(3):
        for k in range(4):
            pair_copy(p, k).wait_send()
        for d in range(2):
            for kind in range(3):
                for copy in copies1(p, d, kind):
                    copy.wait_send()
        for k in (1, 2, 3):
            for copy in copies2(p, k) + copies3(p, k):
                copy.wait_send()
    for copy in reduce_copies:
        copy.wait_send()


def scratch():
    f32, bf16, i16 = jnp.float32, jnp.bfloat16, jnp.int16

    def each(shape, dtype):
        return [pltpu.VMEM(shape(n), dtype) for n in ROWS]

    shapes = [
        pltpu.VMEM((1024, GROUP, 128), bf16),
        pltpu.VMEM((3, 64, 128), f32),
        pltpu.VMEM((256, 128), f32),
        pltpu.VMEM((4, 8, 128), f32),
        pltpu.VMEM((4, 3, 8, 128), f32),
    ]
    shapes += each(lambda n: (4, 16, n, 128), bf16) * 2
    shapes += each(lambda n: (2, 8, n, 128), f32) * 2
    shapes += each(lambda n: (2, 8, 128), f32) * 2
    shapes += each(lambda n: (2, 3, 8, n, 128), i16) * 2
    shapes += each(lambda n: (2, 3, 2, 8, 128), f32) * 2
    shapes += each(lambda n: (4, n, 128), f32)
    shapes += each(lambda n: (8, 128), f32)
    shapes += each(lambda n: (3, 4, n, 128), i16) * 2
    shapes += each(lambda n: (3, 2, 8, 128), f32) * 2
    shapes += each(lambda n: (3, n, 128), i16) * 2
    shapes += each(lambda n: (3, 8, 128), f32) * 2
    dma = pltpu.SemaphoreType.DMA
    shapes += [dma((LOADS,)), dma((3, 4, 2)), dma((2,)), dma((3, 2, 3, 2, 2)), dma((3, 3, 2, 2)),
               dma((3, 3, 2, 2)), dma((4, 3, 2))]
    return shapes


def local(mantissa, scales, counts, owner_map):
    position = jnp.arange(512, dtype=jnp.int32)
    live = counts[:, None] > position[None, :]
    lived = jnp.where(live, scales.reshape(64, 512).astype(jnp.float32), 0.0).reshape(1024, GROUP)
    ordered = jnp.take(lived, owner_map, axis=0).reshape(64, 2, 256).transpose(1, 0, 2)
    scale = jnp.stack(
        [jnp.pad(ordered[:, :, s : s + n], ((0, 0), (0, 0), (0, 128 - n))) for s, n in zip(START, ROWS)], axis=1
    )
    vmem = pl.BlockSpec(memory_space=pltpu.VMEM)
    out, peak = pl.pallas_call(
        kernel,
        out_shape=(jax.ShapeDtypeStruct((256, 128), jnp.bfloat16), jax.ShapeDtypeStruct((2, 128), jnp.float32)),
        in_specs=[pl.BlockSpec(memory_space=pltpu.SMEM), pl.BlockSpec(memory_space=pl.ANY), vmem, vmem],
        out_specs=(vmem, vmem),
        scratch_shapes=scratch(),
        compiler_params=pltpu.CompilerParams(
            collective_id=0, has_side_effects=True, vmem_limit_bytes=60 * 1024 * 1024
        ),
    )(owner_map, mantissa.reshape(1024, GROUP, 128), scale, jnp.eye(128, dtype=jnp.float32))
    return out, peak.reshape(256)


def solution(mesh):
    return jax.shard_map(
        local,
        mesh=mesh,
        in_specs=(P(AXES, None), P(AXES), P(AXES), P()),
        out_specs=(P(AXES, None), P(AXES)),
        check_vma=False,
    )
```

time: 247 us -> 66.4 us (0.27)
  blocking collectives: 164 us -> 0 us
  Pallas kernels: 0 us -> 53.7 us
  starting transfers between devices: 26.8 us -> 0 us
  local copies, waits for them, and re-layouts: 26.8 us -> 7.99 us
  other arithmetic: 22.2 us -> 3.6 us
  waiting for transfers between devices: 3.29 us -> 0 us
    all_to_all x1 -> x0, blocking collectives: 59.5 us -> none  [grouped_exchange(): lax.all_to_all(group, axis, split_axis=split_dim, concat_axis=concat_dim,...]
    pallas_call x0 -> x1, Pallas kernels: none -> 53.7 us  [local(): pl.pallas_call(kernel, out_shape=(jax.ShapeDtypeStruct((256, 128), jnp.bf...]
    all_gather x3 -> x0, blocking collectives: 51.4 us -> none  [gather_in_order(): tiles = lax.all_gather(tiles, axes[k])]
    psum x4 -> x0, blocking collectives: 30.6 us -> none  [one_axis_at_a_time(): shard = lax.psum(shard, axis)]
    all_to_all x3 -> x0, starting transfers between devices: 26.8 us -> none  [grouped_exchange(): lax.all_to_all(group, axis, split_axis=split_dim, concat_axis=concat_dim,...]
    unnamed x1 -> x0, blocking collectives: 22.1 us -> none
    gather x5 -> x2, local copies, waits for them, and re-layouts: 17.5 us -> 3.04 us  [local(): jnp.take(lived, owner_map, axis=0).reshape(64, 2, 256).transpose(1, 0, 2)]
    reduce_sum x4 -> x0, other arithmetic: 9.69 us -> none  [the longest x2 8.77 us: sum_sources(): jnp.sum(values.astype(jnp.float32) * weights.astype(jnp.float32)[:, :, No...]
  transfers between devices with their start and end apart: 3 -> 0, of which waited for: 1 -> 0; matrix products, arithmetic and copies ran while one was open for 14% -> 0% of each run, Pallas kernels for 0% -> 0%
where the time goes in v1:
time: 66.4 us; the launch traced here: 66 us
  Pallas kernels  53.7 us (81%)
  local copies, waits for them, and re-layouts  7.99 us (12%)
  other arithmetic  3.6 us (5%)
  between operations  0.72 us (1%)
    pallas_call x1, Pallas kernels, local(): pl.pallas_call(kernel, out_shape=(jax.ShapeDtypeStruct((256, 128), jnp.bf...  53.7 us
    gather x2, local copies, waits for them, and re-layouts, local(): jnp.take(lived, owner_map, axis=0).reshape(64, 2, 256).transpose(1, 0, 2)  3.04 us
    unnamed x2, local copies, waits for them, and re-layouts  2.71 us
    another operation x2, other arithmetic, local(): jnp.stack([jnp.pad(ordered[:, :, s:s + n], ((0, 0), (0, 0), (0, 128 - n))...  1.34 us

profile of v1, /device:TPU:0, one launch (start us, length us, event | category | flops | bytes accessed | tf_op | source)
XLA Modules:
  0.0 66.0 jit_solution(3392785979267659186)
XLA Ops:
  0.6 1.0 %reshape.31 = f32[1024,32]{1,0:T(8,128)S(1)} reshape(bf16[32768]{0:T(1024)(128)(2,1)} %param.5) | data formatting | bytes 196608 | tf_op jit(solution)/shard_map/convert_element_type | solution.py:348
  1.6 0.7 %gt.26 = s32[64,16]{1,0:T(8,128)S(1)} broadcast(s32[64]{0:T(128)} %param.6), dimensions={0} | broadcast | bytes 4352 | tf_op jit(solution)/shard_map/gt | solution.py:347
  2.3 0.1 gt.27
  2.4 0.2 fusion
  2.6 0.7 %fusion.4 = s32[1024]{0:T(1024)S(1)} fusion(s32[1024]{0:T(1024)} %owner.1), kind=kLoop, calls=%fused_computation.15 | loop fusion | flops 4096 | bytes 8192 | tf_op jit(solution)/shard_map/jit(_take)/gather | solution.py:349
  3.3 2.8 %gather_fusion = f32[1024,32]{1,0:T(8,128)S(1)} fusion(f32[1024,32]{1,0:T(8,128)S(1)} %fusion, s32[1024]{0:T(1024)S(1)} %fusion.4), kind=kCustom, calls=%fused_computation | custom fusion | bytes 266240 | tf_op jit(solution)/shard_map/jit(_take)/gather | solution.py:349
  6.1 0.2 gather.7
  6.4 0.7 %compare_and_fusion = pred[1024]{0:T(1024)(128)(4,1)S(1)} fusion(s32[1024]{0:T(1024)} %owner.1), kind=kLoop, calls=%fused_computation.14 | loop fusion | flops 6144 | bytes 5120 | tf_op jit(solution)/shard_map/jit(_take)/and | solution.py:349
  7.1 0.1 broadcast_in_dim.22
  7.2 0.1 copy.8
  7.3 0.1 copy.9
  7.5 0.1 fusion.5
  7.6 0.7 %fusion.2 = f32[2,1,64,128]{3,2,1,0:T(8,128)S(1)} fusion(f32[2,64,256]{2,1,0:T(8,128)S(1)} %fusion.1, pred[128]{0:T(512)(128)(4,1)} %constant.17.clone.1), kind=kLoop, calls=%fused_computation.7 | loop fusion | flops 16384 | bytes 131200 | tf_op jit(solution)/shard_map/stack | solution.py:350
  8.3 0.7 %pad_maximum_fusion.scale = f32[2,3,64,128]{3,2,1,0:T(8,128)} fusion(f32[2,1,64,128]{3,2,1,0:T(8,128)S(1)} %get-tuple-element.8, f32[2,1,64,128]{3,2,1,0:T(8,128)S(1)} %get-tuple-element.9, f32[2,1,64,128]{3,2,1,0:T(8,128)S(1)} %fusion.2), kind=kLoop, calls=%fused_computation.3 | loop fusion | flops 98304 | bytes 393216 | tf_op jit(solution)/shard_map/stack | solution.py:350
  8.9 0.6 fusion.3.eye
  9.6 53.7 %shard_map.59 = (bf16[256,128]{1,0:T(8,128)(2,1)}, f32[2,128]{1,0:T(2,128)}) custom-call(s32[1024]{0:T(1024)} %owner.1, bf16[1024,32,128]{2,1,0:T(8,128)(2,1)} %bitcast.19, f32[2,3,64,128]{3,2,1,0:T(8,128)} %pad_maximum_fusion.scale, f32[128,128]{1,0:T(8,128)} %fusion.3.eye), custom_call_target="tpu_custom_call" | custom-call | tf_op jit(solution)/shard_map/pallas_call | solution.py:354
  63.3 1.5 %copy.18 = bf16[256,128]{1,0:T(8,128)(2,1)} copy(bf16[256,128]{1,0:T(8,128)(2,1)} %get-tuple-element.12) | data formatting | bytes 131072
  64.8 1.2 %copy.19 = f32[256]{0:T(256)} copy(f32[256]{0:T(256)} %bitcast.21) | data formatting | bytes 2048
  (4 shorter events, 0.1 us)

commit v2 on v1

v2 whole, which is shorter than its diff:
```python
import jax
import jax.numpy as jnp
from jax import lax
from jax.experimental import pallas as pl
from jax.experimental.pallas import tpu as pltpu
from jax.sharding import PartitionSpec as P

MESH = pl.DeviceIdType.MESH
AXES = ("expert", "replica")
GROUP = 32
CLIP = 0.05
EPS = 1e-06
ROWS = (96, 80, 80)
START = (0, 96, 176)
PIECES = (
    ((0, 0, 32), (1, 0, 32), (2, 0, 32)),
    ((3, 0, 32), (4, 0, 32), (5, 0, 16)),
    ((5, 16, 16), (6, 0, 32), (7, 0, 32)),
)
ORDER = (2, 1, 3, 0)
BATCHES = 2
WIDTH = 4 // BATCHES
FAR, OWN, BOTH = 0, 1, 2
TOP = 32767.0
LOADS = 8


def pick(k, a, b, c):
    return a * ((1 - k) * (2 - k) // 2) + b * (k * (2 - k)) + c * (k * (k - 1) // 2)


def kernel(owner, counts, mant_hbm, scales, count_row, avg, total_out, *rest):
    rest = list(rest)

    def take(n):
        head = rest[:n]
        del rest[:n]
        return head

    mant, eye, lived, far_lived, turned, lines, far_lines = take(7)
    tile, tiles, table, times, red_send, red_near, red_far = take(7)
    dsend, drecv, own = take(3), take(3), take(3)
    q1, r1, t1, u1 = take(3), take(3), take(3), take(3)
    mid = take(3)
    q2, r2, t2, u2 = take(3), take(3), take(3), take(3)
    q3, r3, t3, u3 = take(3), take(3), take(3), take(3)
    load_sem, pair_sem, fs_sem, sem1, sem2, sem3, near_sem, far_sem = rest

    e, r = lax.axis_index("expert"), lax.axis_index("replica")
    z, x = lax.div(e, 4), lax.rem(e, 4)
    y, core = lax.div(r, 2), lax.rem(r, 2)
    partner = (e, y * 2 + 1 - core)

    def moved(c, p, ra, rb, rc):
        first = lax.rem(p + c, 3)
        dx, dy, dz = (pick(lax.rem(dim + 3 - first, 3), ra, rb, rc) for dim in range(3))
        return lax.rem(x + dx, 4), lax.rem(y + dy, 4), lax.rem(z + dz, 4)

    def first_group(c, p, ra, rb, rc):
        x2, y2, z2 = moved(c, p, ra, rb, rc)
        return (((z2 * 4 + x2) * 4 + y2) * 2 + c) * 8

    def peer(p, role, rel):
        rels = [0, 0, 0]
        rels[role] = rel
        x2, y2, z2 = moved(core, p, *rels)
        return (z2 * 4 + x2, y2 * 2 + core)

    def remote(src, dst, sems, device):
        return pltpu.make_async_remote_copy(
            src_ref=src, dst_ref=dst, send_sem=sems.at[0], recv_sem=sems.at[1],
            device_id=device, device_id_type=MESH,
        )

    def load(i):
        part = pl.ds(i * (1024 // LOADS), 1024 // LOADS)
        return pltpu.make_async_copy(mant_hbm.at[part], mant.at[part], load_sem.at[i])

    for i in range(LOADS):
        load(i).start()

    near_peers = [(e, lax.rem(r + j, 8)) for j in range(1, 8)]
    far_peers = [(lax.rem(e + j, 16), r) for j in range(1, 16)]
    barrier = pltpu.get_barrier_semaphore()
    for device in near_peers + far_peers:
        pl.semaphore_signal(barrier, inc=1, device_id=device, device_id_type=MESH)

    row16 = lax.broadcasted_iota(jnp.int32, (16, 128), 0)
    lane16 = lax.broadcasted_iota(jnp.int32, (16, 128), 1)
    spot = lane16 + lax.rem(row16, 4) * 128
    which = lax.div(row16, 4)

    @pl.loop(0, 16)
    def _(b):
        bound = jnp.where(which < 2, jnp.where(which == 0, counts[b * 4], counts[b * 4 + 1]),
                          jnp.where(which == 2, counts[b * 4 + 2], counts[b * 4 + 3]))
        rows = pl.ds(pl.multiple_of(b * 16, 16), 16)
        lived[rows] = jnp.where(spot < bound, scales[rows].astype(jnp.float32), 0.0)

    def expand(source, target):
        for q in range(4):
            turned[q] = source[...] if q == 0 else pltpu.roll(source[...], 128 - q * GROUP, 1)

        @pl.loop(0, 32)
        def _(b):
            for i in range(8):
                for q in range(4):
                    target[(b * 8 + i) * 4 + q] = turned[q, pl.ds(b * 8 + i, 1)]

    eye[...] = jnp.where(
        lax.broadcasted_iota(jnp.int32, (128, 128), 0) == lax.broadcasted_iota(jnp.int32, (128, 128), 1), 1.0, 0.0
    )
    row8 = lax.broadcasted_iota(jnp.int32, (8, 128), 0)
    tile[...] = jnp.where(row8 == r, jnp.broadcast_to(count_row[...].astype(jnp.float32), (8, 128)), 0.0)
    pl.semaphore_wait(barrier, 22)

    fs_copy = remote(lived, far_lived, fs_sem, partner)
    fs_copy.start()
    count_near = [remote(tile, tiles.at[j], near_sem.at[0, j], near_peers[j]) for j in range(7)]
    count_far = [remote(table.at[e], table.at[e], far_sem.at[0, j], far_peers[j]) for j in range(15)]
    for copy in count_near:
        copy.start()
    expand(lived, lines)
    for i in range(LOADS):
        load(i).wait()

    def pair_copy(p, k, bat):
        part = pl.ds(bat * WIDTH * 4, WIDTH * 4)
        return remote(dsend[p].at[k, part], drecv[p].at[k, part], pair_sem.at[p, k, bat], partner)

    def gather(bat, k):
        for p in range(3):

            @pl.loop(0, WIDTH)
            def _(w):
                c = bat * WIDTH + w
                rc = 2 - c + pick(lax.div(c, 2), 0, 3, 0) - pick(lax.rem(c, 2) * lax.div(c, 2), 0, 2, 0)
                for rb in range(4):
                    first = first_group(1 - core, p, ORDER[k], rb, rc)
                    at = 0
                    for g, r0, n in PIECES[p]:
                        dsend[p][k, c * 4 + rb, pl.ds(at, n)] = mant[owner[first + g], pl.ds(r0, n)]
                        at += n

            pair_copy(p, k, bat).start()

    def column(row, n):
        return jnp.sum(row * eye[pl.ds(0, n)], axis=1, keepdims=True)

    def product(p, k, rb, c):
        first = first_group(core, p, ORDER[k], rb, ORDER[c])
        values, at = [], 0
        for g, r0, n in PIECES[p]:
            group = owner[first + g]
            chosen = eye[pl.ds(r0, n)]
            s1 = jnp.sum(lines[group] * chosen, axis=1, keepdims=True)
            s2 = jnp.sum(far_lines[group] * chosen, axis=1, keepdims=True)
            mine = mant[group, pl.ds(r0, n)].astype(jnp.float32)
            other = drecv[p][k, c * 4 + rb, pl.ds(at, n)].astype(jnp.float32)
            values.append(mine * s1 + other * s2)
            at += n
        return jnp.concatenate(values, axis=0)

    def quantize(v):
        n = v.shape[0]
        most = jnp.maximum(jnp.max(jnp.abs(v), axis=1, keepdims=True), 1e-30)
        q = lax.round(v * (TOP / most), lax.RoundingMethod.TO_NEAREST_EVEN)
        step = jnp.sum((most * (1.0 / TOP)) * eye[pl.ds(0, n)], axis=0, keepdims=True)
        return q.astype(jnp.int32).astype(jnp.int16), step

    def restored(q, row):
        return q.astype(jnp.int32).astype(jnp.float32) * column(row, q.shape[0])

    def copies1(p, d, kind, bat):
        device = peer(p, 0, 1 + 2 * d)
        part = pl.ds(bat * WIDTH * 2, WIDTH * 2)
        return (
            remote(q1[p].at[d, kind, part], r1[p].at[d, kind, part], sem1.at[p, d, kind, bat, 0], device),
            remote(t1[p].at[d, kind, bat], u1[p].at[d, kind, bat], sem1.at[p, d, kind, bat, 1], device),
        )

    def places(bat):
        return [(c, i) for c in range(bat * WIDTH, (bat + 1) * WIDTH) for i in range(2)]

    def first_dim(bat, kind):
        for p in range(3):
            if kind == FAR:
                pair_copy(p, 0, bat).wait_recv()
            if kind == OWN:
                pair_copy(p, 1, bat).wait_recv()
                pair_copy(p, 2, bat).wait_recv()
            if kind == BOTH:
                for d in range(2):
                    for copy in copies1(p, d, FAR, bat):
                        copy.wait_recv()
            coded = []
            for d in range(2):
                half = 1 - d if kind == OWN else d
                for j, (c, i) in enumerate(places(bat)):
                    v = product(p, 0 if kind == FAR else 1 + d, half * 2 + i, c)
                    if kind == BOTH:
                        v = v + restored(r1[p][d, FAR, c * 2 + i], u1[p][d, FAR, bat, pl.ds(j, 1)])
                    coded.append((d, c * 2 + i, j, quantize(v)))
            for d, u, j, (q, step) in coded:
                q1[p][d, kind, u] = q
                t1[p][d, kind, bat, pl.ds(j, 1)] = step
            for d in range(2):
                for copy in copies1(p, d, kind, bat):
                    copy.start()

    def own_share(bat):
        for p in range(3):
            pair_copy(p, 3, bat).wait_recv()
            for c in range(bat * WIDTH, (bat + 1) * WIDTH):
                values = [product(p, 3, rb, c) for rb in range(4)]
                for rb in range(4):
                    own[p][c * 4 + rb] = values[rb]

    def copies2(p, k, bat):
        device = peer(p, 1, k)
        part = pl.ds(bat * WIDTH, WIDTH)
        return (
            remote(q2[p].at[k - 1, part], r2[p].at[k - 1, part], sem2.at[p, k - 1, bat, 0], device),
            remote(t2[p].at[k - 1, bat], u2[p].at[k - 1, bat], sem2.at[p, k - 1, bat, 1], device),
        )

    def second_dim(bat):
        for p in range(3):
            for d in range(2):
                for kind in (OWN, BOTH):
                    for copy in copies1(p, d, kind, bat):
                        copy.wait_recv()
            for rb in ORDER:
                h, values = rb // 2, []
                for w in range(WIDTH):
                    c = bat * WIDTH + w
                    v = own[p][c * 4 + rb]
                    for d, kind in ((h, BOTH), (1 - h, OWN)):
                        v = v + restored(r1[p][d, kind, c * 2 + rb % 2], u1[p][d, kind, bat, pl.ds(w * 2 + rb % 2, 1)])
                    values.append(v)
                if rb:
                    for w, v in enumerate(values):
                        q2[p][rb - 1, bat * WIDTH + w], t2[p][rb - 1, bat, pl.ds(w, 1)] = quantize(v)
                    for copy in copies2(p, rb, bat):
                        copy.start()
                else:
                    for w, v in enumerate(values):
                        mid[p][bat * WIDTH + w] = v

    def copies3(p, k):
        device = peer(p, 2, k)
        return (
            remote(q3[p].at[k - 1], r3[p].at[k - 1], sem3.at[p, k - 1, 0], device),
            remote(t3[p].at[k - 1], u3[p].at[k - 1], sem3.at[p, k - 1, 1], device),
        )

    def third_dim(bat):
        for p in range(3):
            for k in (1, 3, 2):
                for copy in copies2(p, k, bat):
                    copy.wait_recv()
            values = []
            for w in range(WIDTH):
                c = bat * WIDTH + w
                v = mid[p][c]
                for k in range(3):
                    v = v + restored(r2[p][k, c], u2[p][k, bat, pl.ds(w, 1)])
                values.append(v)
            for w, v in enumerate(values):
                rc = ORDER[bat * WIDTH + w]
                if rc:
                    q3[p][rc - 1], t3[p][rc - 1, pl.ds(0, 1)] = quantize(v)
                    for copy in copies3(p, rc):
                        copy.start()
                else:
                    mid[p][3] = v

    def count_sources():
        for copy in count_far:
            copy.wait_recv()
        loads = table[...].reshape(128, 128).T[:64]
        expert = lax.broadcasted_iota(jnp.int32, (64, 128), 0)
        first = (e * 8 + r) * 8
        found = []
        for g in range(8):
            group = owner[first + g]
            place = lax.broadcasted_iota(jnp.int32, (GROUP, 128), 0) + lax.rem(group, 16) * GROUP
            load_line = jnp.sum(jnp.where(expert == lax.div(group, 16), loads, 0.0), axis=0, keepdims=True)
            live = jnp.where(load_line > place.astype(jnp.float32), 1.0, 0.0)
            found.append(jnp.maximum(jnp.sum(live, axis=1, keepdims=True), 1.0))
        for g in range(8):
            times[pl.ds(g * GROUP, GROUP)] = jnp.broadcast_to(found[g], (GROUP, 128))

    for k in (0, 1, 2):
        gather(0, k)
    fs_copy.wait_recv()
    expand(far_lived, far_lines)
    first_dim(0, FAR)
    for k in (0, 1, 2):
        gather(1, k)
    first_dim(0, OWN)
    mine = tile[...]
    for j, copy in enumerate(count_near):
        copy.wait_recv()
        mine = mine + tiles[j]
    table[e] = mine
    for copy in count_far:
        copy.start()
    first_dim(1, FAR)
    gather(0, 3)
    first_dim(0, BOTH)
    gather(1, 3)
    first_dim(1, OWN)
    own_share(0)
    first_dim(1, BOTH)
    own_share(1)
    second_dim(0)
    second_dim(1)
    count_sources()
    third_dim(0)
    third_dim(1)

    square = jnp.zeros((8, 128), jnp.float32)
    for p in range(3):
        n = ROWS[p]
        for k in (1, 3, 2):
            for copy in copies3(p, k):
                copy.wait_recv()
        v = mid[p][3]
        for k in range(3):
            v = v + restored(r3[p][k], u3[p][k, pl.ds(0, 1)])
        mean = v / times[pl.ds(START[p], n)]
        avg[pl.ds(START[p], n)] = mean
        square = square + jnp.sum((mean * mean).reshape(n // 8, 8, 128), axis=0)

    red_send[0] = square
    red_copies = [remote(red_send.at[0], red_near.at[j], near_sem.at[1, j], near_peers[j]) for j in range(7)]
    for copy in red_copies:
        copy.start()
    for j, copy in enumerate(red_copies):
        copy.wait_recv()
        square = square + red_near[j]
    red_send[1] = square
    red_copies2 = [remote(red_send.at[1], red_far.at[j], far_sem.at[1, j], far_peers[j]) for j in range(15)]
    for copy in red_copies2:
        copy.start()
    for j, copy in enumerate(red_copies2):
        copy.wait_recv()
        square = square + red_far[j]
    total_out[...] = square

    fs_copy.wait_send()
    for copy in count_near + count_far + red_copies + red_copies2:
        copy.wait_send()
    for p in range(3):
        for bat in range(BATCHES):
            for k in range(4):
                pair_copy(p, k, bat).wait_send()
            for d in range(2):
                for kind in range(3):
                    for copy in copies1(p, d, kind, bat):
                        copy.wait_send()
            for k in (1, 2, 3):
                for copy in copies2(p, k, bat):
                    copy.wait_send()
        for k in (1, 2, 3):
            for copy in copies3(p, k):
                copy.wait_send()


def scratch():
    f32, bf16, i16 = jnp.float32, jnp.bfloat16, jnp.int16

    def each(shape, dtype):
        return [pltpu.VMEM(shape(n), dtype) for n in ROWS]

    shapes = [
        pltpu.VMEM((1024, GROUP, 128), bf16),
        pltpu.VMEM((128, 128), f32),
        pltpu.VMEM((256, 128), f32),
        pltpu.VMEM((256, 128), f32),
        pltpu.VMEM((4, 256, 128), f32),
        pltpu.VMEM((1024, 1, 128), f32),
        pltpu.VMEM((1024, 1, 128), f32),
        pltpu.VMEM((8, 128), f32),
        pltpu.VMEM((7, 8, 128), f32),
        pltpu.VMEM((16, 8, 128), f32),
        pltpu.VMEM((256, 128), f32),
        pltpu.VMEM((2, 8, 128), f32),
        pltpu.VMEM((7, 8, 128), f32),
        pltpu.VMEM((15, 8, 128), f32),
    ]
    shapes += each(lambda n: (4, 16, n, 128), bf16) * 2
    shapes += each(lambda n: (16, n, 128), f32)
    shapes += each(lambda n: (2, 3, 8, n, 128), i16) * 2
    shapes += each(lambda n: (2, 3, BATCHES, 8, 128), f32) * 2
    shapes += each(lambda n: (4, n, 128), f32)
    shapes += each(lambda n: (3, 4, n, 128), i16) * 2
    shapes += each(lambda n: (3, BATCHES, 8, 128), f32) * 2
    shapes += each(lambda n: (3, n, 128), i16) * 2
    shapes += each(lambda n: (3, 8, 128), f32) * 2
    dma = pltpu.SemaphoreType.DMA
    shapes += [dma((LOADS,)), dma((3, 4, BATCHES, 2)), dma((2,)), dma((3, 2, 3, BATCHES, 2, 2)),
               dma((3, 3, BATCHES, 2, 2)), dma((3, 3, 2, 2)), dma((2, 7, 2)), dma((2, 15, 2))]
    return shapes


def local(mantissa, scales, counts, owner_map):
    vmem, smem = pl.BlockSpec(memory_space=pltpu.VMEM), pl.BlockSpec(memory_space=pltpu.SMEM)
    averaged, square = pl.pallas_call(
        kernel,
        out_shape=(jax.ShapeDtypeStruct((256, 128), jnp.float32), jax.ShapeDtypeStruct((8, 128), jnp.float32)),
        in_specs=[smem, smem, pl.BlockSpec(memory_space=pl.ANY), vmem, vmem],
        out_specs=(vmem, vmem),
        scratch_shapes=scratch(),
        compiler_params=pltpu.CompilerParams(
            collective_id=0, has_side_effects=True, vmem_limit_bytes=60 * 1024 * 1024
        ),
    )(owner_map, counts, mantissa.reshape(1024, GROUP, 128), scales.reshape(256, 128), jnp.pad(counts, (0, 64)).reshape(1, 128))
    root_mean = jnp.sqrt(jnp.sum(square) / (32768 * 128) + EPS)
    clipped = averaged * jnp.minimum(1.0, CLIP / root_mean)
    top = jnp.max(jnp.abs(clipped), axis=1) + EPS
    return (clipped / top[:, None]).astype(jnp.bfloat16), top


def solution(mesh):
    return jax.shard_map(
        local,
        mesh=mesh,
        in_specs=(P(AXES, None), P(AXES), P(AXES), P()),
        out_specs=(P(AXES, None), P(AXES)),
        check_vma=False,
    )
```

time: 66.4 us -> 59.3 us (0.89)
  local copies, waits for them, and re-layouts: 7.99 us -> 1.18 us
  Pallas kernels: 53.7 us -> 52.2 us
    gather x2 -> x0, local copies, waits for them, and re-layouts: 3.04 us -> none  [local(): jnp.take(lived, owner_map, axis=0).reshape(64, 2, 256).transpose(1, 0, 2)]
    unnamed x2, local copies, waits for them, and re-layouts: 2.71 us -> 0.01 us
    pallas_call x1, Pallas kernels: 53.7 us -> 52.2 us  [local(): pl.pallas_call(kernel, out_shape=(jax.ShapeDtypeStruct((256, 128), jnp.fl...]
    another operation x2 -> x0, other arithmetic: 1.34 us -> none  [local(): jnp.stack([jnp.pad(ordered[:, :, s:s + n], ((0, 0), (0, 0), (0, 128 - n))...]
    reduce_sum x0 -> x1, other arithmetic: none -> 1.28 us  [local(): root_mean = jnp.sqrt(jnp.sum(square) / (32768 * 128) + EPS)]
    reshape x0 -> x1, local copies, waits for them, and re-layouts: none -> 1.17 us  [local(): jnp.pad(counts, (0, 64)).reshape(1, 128)]
    reduce_max x0 -> x1, other arithmetic: none -> 1.02 us  [local(): top = jnp.max(jnp.abs(clipped), axis=1) + EPS]
    convert_element_type x1, other arithmetic: 0.64 us -> 1.64 us  [local(): return ((clipped / top[:, None]).astype(jnp.bfloat16), top)]
where the time goes in v2:
time: 59.3 us; the launch traced here: 58.6 us
  Pallas kernels  52.2 us (88%)
  other arithmetic  3.94 us (7%)
  between operations  1.35 us (2%)
  local copies, waits for them, and re-layouts  1.18 us (2%)
    pallas_call x1, Pallas kernels, local(): pl.pallas_call(kernel, out_shape=(jax.ShapeDtypeStruct((256, 128), jnp.fl...  52.2 us
    convert_element_type x1, other arithmetic, local(): return ((clipped / top[:, None]).astype(jnp.bfloat16), top)  1.64 us
    reduce_sum x1, other arithmetic, local(): root_mean = jnp.sqrt(jnp.sum(square) / (32768 * 128) + EPS)  1.28 us

profile of v2, /device:TPU:0, one launch (start us, length us, event | category | flops | bytes accessed | tf_op | source)
XLA Modules:
  0.0 58.6 jit_solution(6011226900716867836)
XLA Ops:
  0.6 1.2 %pad_bitcast_fusion.count_row = s32[1,128]{1,0:T(1,128)} fusion(s32[64]{0:T(128)} %counts.1), kind=kLoop, calls=%fused_computation.3 | loop fusion | bytes 768 | tf_op jit(solution)/shard_map/reshape | solution.py:419
  1.8 52.2 %shard_map.59 = (f32[256,128]{1,0:T(8,128)}, f32[8,128]{1,0:T(8,128)}) custom-call(s32[1024]{0:T(1024)} %owner.1, s32[64]{0:T(128)} %counts.1, bf16[1024,32,128]{2,1,0:T(8,128)(2,1)} %bitcast.4, bf16[256,128]{1,0:T(8,128)(2,1)} %bitcast.5, s32[1,128]{1,0:T(1,128)} %pad_bitcast_fusion.count_row), custom_call_target="tpu_custom_call" | custom-call | tf_op jit(solution)/shard_map/pallas_call | solution.py:410
  54.0 1.3 %reduce_sum.9 = f32[]{:T(128)} reduce(f32[8,128]{1,0:T(8,128)} %get-tuple-element.5, f32[]{:T(128)} %constant.2.clone.1), dimensions={0,1}, to_apply=%region_0.1 | reduce | flops 1023 | bytes 4104 | tf_op jit(solution)/shard_map/reduce_sum | solution.py:420
  55.9 1.0 %abs_reduce_fusion = f32[256]{0:T(256)S(1)} fusion(f32[256,128]{1,0:T(8,128)} %get-tuple-element.4, f32[]{:T(128)S(6)} %min_shard_map.3), kind=kLoop, calls=%fused_computation.1 | loop fusion | flops 98048 | bytes 132100 | tf_op jit(solution)/shard_map/reduce_max | solution.py:422
  57.0 0.0 copy-start
  57.0 1.6 %divide_convert_fusion = bf16[256,128]{1,0:T(8,128)(2,1)} fusion(f32[256,128]{1,0:T(8,128)} %get-tuple-element.4, f32[256]{0:T(256)S(1)} %broadcast_add_fusion, f32[]{:T(128)S(6)} %min_shard_map.3), kind=kLoop, calls=%fused_computation | loop fusion | flops 98304 | bytes 197636 | tf_op jit(solution)/shard_map/convert_element_type | solution.py:423
  58.6 0.0 copy-done
  (1 shorter events, 0.0 us)
Async XLA Ops:
  57.0 1.7 %copy-start = (f32[256]{0:T(256)}, f32[256]{0:T(256)S(1)}, u32[]{:S(2)}) copy-start(f32[256]{0:T(256)S(1)} %broadcast_add_fusion) | copy-start | bytes 3076

commit v3 on v2

--- a/solution.py
+++ b/solution.py
@@ -29,7 +29,7 @@
     return a * ((1 - k) * (2 - k) // 2) + b * (k * (2 - k)) + c * (k * (k - 1) // 2)
 
 
-def kernel(owner, counts, mant_hbm, scales, count_row, avg, total_out, *rest):
+def kernel(owner, counts, mant_hbm, scales, count_row, out, peak, *rest):
     rest = list(rest)
 
     def take(n):
@@ -38,7 +38,7 @@
         return head
 
     mant, eye, lived, far_lived, turned, lines, far_lines = take(7)
-    tile, tiles, table, times, red_send, red_near, red_far = take(7)
+    tile, tiles, table, times, red_send, red_near, red_far, avg = take(8)
     dsend, drecv, own = take(3), take(3), take(3)
     q1, r1, t1, u1 = take(3), take(3), take(3), take(3)
     mid = take(3)
@@ -51,19 +51,27 @@
     y, core = lax.div(r, 2), lax.rem(r, 2)
     partner = (e, y * 2 + 1 - core)
 
-    def moved(c, p, ra, rb, rc):
-        first = lax.rem(p + c, 3)
-        dx, dy, dz = (pick(lax.rem(dim + 3 - first, 3), ra, rb, rc) for dim in range(3))
-        return lax.rem(x + dx, 4), lax.rem(y + dy, 4), lax.rem(z + dz, 4)
+    turns = [[lax.rem(v + rel, 4) for rel in range(4)] for v in (x, y, z)]
+    weights = (64, 16, 256)
+
+    def turned_by(c):
+        return [
+            [pick(lax.rem(dim + c, 3), *(turns[i][rel] * weights[i] for i in range(3))) for rel in range(4)]
+            for dim in range(3)
+        ]
+
+    mine_at, other_at = turned_by(core), turned_by(1 - core)
 
     def first_group(c, p, ra, rb, rc):
-        x2, y2, z2 = moved(c, p, ra, rb, rc)
-        return (((z2 * 4 + x2) * 4 + y2) * 2 + c) * 8
+        at = mine_at if c == 0 else other_at
+        own_core = core if c == 0 else 1 - core
+        return at[p][ra] + at[(p + 1) % 3][rb] + at[(p + 2) % 3][rc] + own_core * 8
 
     def peer(p, role, rel):
-        rels = [0, 0, 0]
-        rels[role] = rel
-        x2, y2, z2 = moved(core, p, *rels)
+        dim = lax.rem((p + role) % 3 + core, 3)
+        x2, y2, z2 = (
+            pick(lax.rem(dim + 3 - i, 3), turns[i][rel], turns[i][0], turns[i][0]) for i in range(3)
+        )
         return (z2 * 4 + x2, y2 * 2 + core)
 
     def remote(src, dst, sems, device):
@@ -99,7 +107,8 @@
 
     def expand(source, target):
         for q in range(4):
-            turned[q] = source[...] if q == 0 else pltpu.roll(source[...], 128 - q * GROUP, 1)
+            lanes = source[...] if q == 0 else pltpu.roll(source[...], 128 - q * GROUP, 1)
+            turned[q] = jnp.where(lax.broadcasted_iota(jnp.int32, (256, 128), 1) < GROUP, lanes, 0.0)
 
         @pl.loop(0, 32)
         def _(b):
@@ -111,7 +120,8 @@
         lax.broadcasted_iota(jnp.int32, (128, 128), 0) == lax.broadcasted_iota(jnp.int32, (128, 128), 1), 1.0, 0.0
     )
     row8 = lax.broadcasted_iota(jnp.int32, (8, 128), 0)
-    tile[...] = jnp.where(row8 == r, jnp.broadcast_to(count_row[...].astype(jnp.float32), (8, 128)), 0.0)
+    tile[...] = jnp.zeros((8, 128), jnp.float32)
+    tile[:, pl.ds(0, 64)] = jnp.where(row8[:, :64] == r, jnp.broadcast_to(count_row[...].astype(jnp.float32), (8, 64)), 0.0)
     pl.semaphore_wait(barrier, 22)
 
     fs_copy = remote(lived, far_lived, fs_sem, partner)
@@ -130,46 +140,54 @@
 
     def gather(bat, k):
         for p in range(3):
-
-            @pl.loop(0, WIDTH)
-            def _(w):
-                c = bat * WIDTH + w
-                rc = 2 - c + pick(lax.div(c, 2), 0, 3, 0) - pick(lax.rem(c, 2) * lax.div(c, 2), 0, 2, 0)
+            for c in range(bat * WIDTH, (bat + 1) * WIDTH):
                 for rb in range(4):
-                    first = first_group(1 - core, p, ORDER[k], rb, rc)
+                    first = first_group(1, p, ORDER[k], rb, ORDER[c])
                     at = 0
                     for g, r0, n in PIECES[p]:
                         dsend[p][k, c * 4 + rb, pl.ds(at, n)] = mant[owner[first + g], pl.ds(r0, n)]
                         at += n
-
             pair_copy(p, k, bat).start()
 
-    def column(row, n):
-        return jnp.sum(row * eye[pl.ds(0, n)], axis=1, keepdims=True)
+    lane = lax.broadcasted_iota(jnp.int32, (1, 128), 1)
+
+    def scale_row(source, groups, p):
+        row, at = None, 0
+        for group, (_, r0, n) in zip(groups, PIECES[p]):
+            piece = source[group]
+            if n < GROUP:
+                piece = jnp.where(lane < n, piece, 0.0) if r0 == 0 else jnp.where(lane < r0, 0.0, piece)
+            if at != r0:
+                piece = pltpu.roll(piece, (at - r0) % 128, 1)
+            row = piece if row is None else row + piece
+            at += n
+        return row
+
+    def scaled(row, rows):
+        n = rows.shape[0]
+        weight = (eye[pl.ds(0, n)] * row).astype(jnp.bfloat16)[:, :n]
+        return jnp.dot(weight, rows, preferred_element_type=jnp.float32)
 
     def product(p, k, rb, c):
-        first = first_group(core, p, ORDER[k], rb, ORDER[c])
-        values, at = [], 0
-        for g, r0, n in PIECES[p]:
-            group = owner[first + g]
-            chosen = eye[pl.ds(r0, n)]
-            s1 = jnp.sum(lines[group] * chosen, axis=1, keepdims=True)
-            s2 = jnp.sum(far_lines[group] * chosen, axis=1, keepdims=True)
-            mine = mant[group, pl.ds(r0, n)].astype(jnp.float32)
-            other = drecv[p][k, c * 4 + rb, pl.ds(at, n)].astype(jnp.float32)
-            values.append(mine * s1 + other * s2)
-            at += n
-        return jnp.concatenate(values, axis=0)
+        first = first_group(0, p, ORDER[k], rb, ORDER[c])
+        groups = [owner[first + g] for g, _, _ in PIECES[p]]
+        mine = jnp.concatenate([mant[group, pl.ds(r0, n)] for group, (_, r0, n) in zip(groups, PIECES[p])], axis=0)
+        other = drecv[p][k, c * 4 + rb]
+        return scaled(scale_row(lines, groups, p), mine) + scaled(scale_row(far_lines, groups, p), other)
 
     def quantize(v):
         n = v.shape[0]
         most = jnp.maximum(jnp.max(jnp.abs(v), axis=1, keepdims=True), 1e-30)
-        q = lax.round(v * (TOP / most), lax.RoundingMethod.TO_NEAREST_EVEN)
-        step = jnp.sum((most * (1.0 / TOP)) * eye[pl.ds(0, n)], axis=0, keepdims=True)
-        return q.astype(jnp.int32).astype(jnp.int16), step
+        step = (most * (1.0045 / TOP)).astype(jnp.bfloat16).astype(jnp.float32)
+        q = lax.round(v / step, lax.RoundingMethod.TO_NEAREST_EVEN)
+        row = jnp.sum(step * eye[pl.ds(0, n)], axis=0, keepdims=True)
+        return q.astype(jnp.int32).astype(jnp.int16), row
 
     def restored(q, row):
-        return q.astype(jnp.int32).astype(jnp.float32) * column(row, q.shape[0])
+        n = q.shape[0]
+        weight = (eye[pl.ds(0, n)] * row).astype(jnp.bfloat16)
+        step = jnp.dot(weight, jnp.ones((128, 128), jnp.bfloat16), preferred_element_type=jnp.float32)
+        return q.astype(jnp.int32).astype(jnp.float32) * step
 
     def copies1(p, d, kind, bat):
         device = peer(p, 0, 1 + 2 * d)
@@ -333,21 +351,28 @@
         avg[pl.ds(START[p], n)] = mean
         square = square + jnp.sum((mean * mean).reshape(n // 8, 8, 128), axis=0)
 
-    red_send[0] = square
+    total = jnp.sum(square, axis=0, keepdims=True)
+    red_send[0] = total
     red_copies = [remote(red_send.at[0], red_near.at[j], near_sem.at[1, j], near_peers[j]) for j in range(7)]
     for copy in red_copies:
         copy.start()
     for j, copy in enumerate(red_copies):
         copy.wait_recv()
-        square = square + red_near[j]
-    red_send[1] = square
+        total = total + red_near[j]
+    red_send[1] = total
     red_copies2 = [remote(red_send.at[1], red_far.at[j], far_sem.at[1, j], far_peers[j]) for j in range(15)]
     for copy in red_copies2:
         copy.start()
     for j, copy in enumerate(red_copies2):
         copy.wait_recv()
-        square = square + red_far[j]
-    total_out[...] = square
+        total = total + red_far[j]
+    root_mean = jnp.sqrt(jnp.sum(total, axis=1, keepdims=True) / (32768 * 128) + EPS)
+    factor = jnp.minimum(1.0, CLIP / root_mean)
+    for h in range(2):
+        clipped = avg[pl.ds(h * 128, 128)] * factor
+        top = jnp.max(jnp.abs(clipped), axis=1, keepdims=True) + EPS
+        out[pl.ds(h * 128, 128)] = (clipped / top).astype(jnp.bfloat16)
+        peak[pl.ds(h, 1)] = jnp.sum(top * eye[...], axis=0, keepdims=True)
 
     fs_copy.wait_send()
     for copy in count_near + count_far + red_copies + red_copies2:
@@ -386,9 +411,10 @@
         pltpu.VMEM((7, 8, 128), f32),
         pltpu.VMEM((16, 8, 128), f32),
         pltpu.VMEM((256, 128), f32),
-        pltpu.VMEM((2, 8, 128), f32),
-        pltpu.VMEM((7, 8, 128), f32),
-        pltpu.VMEM((15, 8, 128), f32),
+        pltpu.VMEM((2, 1, 128), f32),
+        pltpu.VMEM((7, 1, 128), f32),
+        pltpu.VMEM((15, 1, 128), f32),
+        pltpu.VMEM((256, 128), f32),
     ]
     shapes += each(lambda n: (4, 16, n, 128), bf16) * 2
     shapes += each(lambda n: (16, n, 128), f32)
@@ -407,20 +433,17 @@
 
 def local(mantissa, scales, counts, owner_map):
     vmem, smem = pl.BlockSpec(memory_space=pltpu.VMEM), pl.BlockSpec(memory_space=pltpu.SMEM)
-    averaged, square = pl.pallas_call(
+    out, peak = pl.pallas_call(
         kernel,
-        out_shape=(jax.ShapeDtypeStruct((256, 128), jnp.float32), jax.ShapeDtypeStruct((8, 128), jnp.float32)),
+        out_shape=(jax.ShapeDtypeStruct((256, 128), jnp.bfloat16), jax.ShapeDtypeStruct((2, 128), jnp.float32)),
         in_specs=[smem, smem, pl.BlockSpec(memory_space=pl.ANY), vmem, vmem],
         out_specs=(vmem, vmem),
         scratch_shapes=scratch(),
         compiler_params=pltpu.CompilerParams(
             collective_id=0, has_side_effects=True, vmem_limit_bytes=60 * 1024 * 1024
         ),
-    )(owner_map, counts, mantissa.reshape(1024, GROUP, 128), scales.reshape(256, 128), jnp.pad(counts, (0, 64)).reshape(1, 128))
-    root_mean = jnp.sqrt(jnp.sum(square) / (32768 * 128) + EPS)
-    clipped = averaged * jnp.minimum(1.0, CLIP / root_mean)
-    top = jnp.max(jnp.abs(clipped), axis=1) + EPS
-    return (clipped / top[:, None]).astype(jnp.bfloat16), top
+    )(owner_map, counts, mantissa.reshape(1024, GROUP, 128), scales.reshape(256, 128), counts.reshape(1, 64))
+    return out, peak.reshape(256)
 
 
 def solution(mesh):

time: 59.3 us -> 53.7 us (0.906)
  other arithmetic: 3.94 us -> 0 us
  Pallas kernels: 52.2 us -> 50.2 us
  local copies, waits for them, and re-layouts: 1.18 us -> 2.67 us
  between operations: 1.35 us -> 0.64 us
    unnamed x2, local copies, waits for them, and re-layouts: 0.01 us -> 2.67 us
    pallas_call x1, Pallas kernels: 52.2 us -> 50.2 us  [local(): pl.pallas_call(kernel, out_shape=(jax.ShapeDtypeStruct((256, 128), jnp.bf...]
    convert_element_type x1 -> x0, other arithmetic: 1.64 us -> none  [local(): return ((clipped / top[:, None]).astype(jnp.bfloat16), top)]
    reduce_sum x1 -> x0, other arithmetic: 1.28 us -> none  [local(): root_mean = jnp.sqrt(jnp.sum(square) / (32768 * 128) + EPS)]
    reshape x1 -> x0, local copies, waits for them, and re-layouts: 1.17 us -> none  [local(): jnp.pad(counts, (0, 64)).reshape(1, 128)]
    reduce_max x1 -> x0, other arithmetic: 1.02 us -> none  [local(): top = jnp.max(jnp.abs(clipped), axis=1) + EPS]
where the time goes in v3:
time: 53.7 us; the launch traced here: 53.5 us
  Pallas kernels  50.2 us (93%)
  local copies, waits for them, and re-layouts  2.67 us (5%)
  between operations  0.64 us (1%)
    pallas_call x1, Pallas kernels, local(): pl.pallas_call(kernel, out_shape=(jax.ShapeDtypeStruct((256, 128), jnp.bf...  50.2 us
    unnamed x2, local copies, waits for them, and re-layouts  2.67 us

profile of v3, /device:TPU:0, one launch (start us, length us, event | category | flops | bytes accessed | tf_op | source)
XLA Modules:
  0.0 53.5 jit_solution(12255554089055538742)
XLA Ops:
  0.6 50.2 %shard_map.59 = (bf16[256,128]{1,0:T(8,128)(2,1)}, f32[2,128]{1,0:T(2,128)}) custom-call(s32[1024]{0:T(1024)} %owner.1, s32[64]{0:T(128)} %counts.1, bf16[1024,32,128]{2,1,0:T(8,128)(2,1)} %bitcast.4, bf16[256,128]{1,0:T(8,128)(2,1)} %bitcast.5, s32[1,64]{1,0:T(1,128)} %bitcast.6), custom_call_target="tpu_custom_call" | custom-call | tf_op jit(solution)/shard_map/pallas_call | solution.py:436
  50.8 1.5 %copy.8 = bf16[256,128]{1,0:T(8,128)(2,1)} copy(bf16[256,128]{1,0:T(8,128)(2,1)} %get-tuple-element.8) | data formatting | bytes 131072
  52.3 1.2 %copy.9 = f32[256]{0:T(256)} copy(f32[256]{0:T(256)} %bitcast.7) | data formatting | bytes 2048

commit v4 on v3

--- a/solution.py
+++ b/solution.py
@@ -29,7 +29,7 @@
     return a * ((1 - k) * (2 - k) // 2) + b * (k * (2 - k)) + c * (k * (k - 1) // 2)
 
 
-def kernel(owner, counts, mant_hbm, scales, count_row, out, peak, *rest):
+def kernel(owner, counts, mant_hbm, scales, count_row, avg, total_out, *rest):
     rest = list(rest)
 
     def take(n):
@@ -38,7 +38,7 @@
         return head
 
     mant, eye, lived, far_lived, turned, lines, far_lines = take(7)
-    tile, tiles, table, times, red_send, red_near, red_far, avg = take(8)
+    tile, tiles, table, times, red_send, red_near, red_far = take(7)
     dsend, drecv, own = take(3), take(3), take(3)
     q1, r1, t1, u1 = take(3), take(3), take(3), take(3)
     mid = take(3)
@@ -287,7 +287,7 @@
             for w, v in enumerate(values):
                 rc = ORDER[bat * WIDTH + w]
                 if rc:
-                    q3[p][rc - 1], t3[p][rc - 1, pl.ds(0, 1)] = quantize(v)
+                    q3[p][rc - 1], t3[p][rc - 1] = quantize(v)
                     for copy in copies3(p, rc):
                         copy.start()
                 else:
@@ -346,7 +346,7 @@
                 copy.wait_recv()
         v = mid[p][3]
         for k in range(3):
-            v = v + restored(r3[p][k], u3[p][k, pl.ds(0, 1)])
+            v = v + restored(r3[p][k], u3[p][k])
         mean = v / times[pl.ds(START[p], n)]
         avg[pl.ds(START[p], n)] = mean
         square = square + jnp.sum((mean * mean).reshape(n // 8, 8, 128), axis=0)
@@ -366,13 +366,7 @@
     for j, copy in enumerate(red_copies2):
         copy.wait_recv()
         total = total + red_far[j]
-    root_mean = jnp.sqrt(jnp.sum(total, axis=1, keepdims=True) / (32768 * 128) + EPS)
-    factor = jnp.minimum(1.0, CLIP / root_mean)
-    for h in range(2):
-        clipped = avg[pl.ds(h * 128, 128)] * factor
-        top = jnp.max(jnp.abs(clipped), axis=1, keepdims=True) + EPS
-        out[pl.ds(h * 128, 128)] = (clipped / top).astype(jnp.bfloat16)
-        peak[pl.ds(h, 1)] = jnp.sum(top * eye[...], axis=0, keepdims=True)
+    total_out[...] = total
 
     fs_copy.wait_send()
     for copy in count_near + count_far + red_copies + red_copies2:
@@ -393,6 +387,17 @@
                 copy.wait_send()
 
 
+def finish(avg, total, out, peak):
+    root_mean = jnp.sqrt(jnp.sum(total[...], axis=1, keepdims=True) / (32768 * 128) + EPS)
+    factor = jnp.minimum(1.0, CLIP / root_mean)
+    same = lax.broadcasted_iota(jnp.int32, (128, 128), 0) == lax.broadcasted_iota(jnp.int32, (128, 128), 1)
+    for h in range(2):
+        clipped = avg[pl.ds(h * 128, 128)] * factor
+        top = jnp.max(jnp.abs(clipped), axis=1, keepdims=True) + EPS
+        out[pl.ds(h * 128, 128)] = (clipped / top).astype(jnp.bfloat16)
+        peak[pl.ds(h, 1)] = jnp.sum(jnp.where(same, top, 0.0), axis=0, keepdims=True)
+
+
 def scratch():
     f32, bf16, i16 = jnp.float32, jnp.bfloat16, jnp.int16
 
@@ -414,17 +419,16 @@
         pltpu.VMEM((2, 1, 128), f32),
         pltpu.VMEM((7, 1, 128), f32),
         pltpu.VMEM((15, 1, 128), f32),
-        pltpu.VMEM((256, 128), f32),
     ]
     shapes += each(lambda n: (4, 16, n, 128), bf16) * 2
     shapes += each(lambda n: (16, n, 128), f32)
     shapes += each(lambda n: (2, 3, 8, n, 128), i16) * 2
-    shapes += each(lambda n: (2, 3, BATCHES, 8, 128), f32) * 2
+    shapes += each(lambda n: (2, 3, BATCHES, WIDTH * 2, 128), f32) * 2
     shapes += each(lambda n: (4, n, 128), f32)
     shapes += each(lambda n: (3, 4, n, 128), i16) * 2
-    shapes += each(lambda n: (3, BATCHES, 8, 128), f32) * 2
+    shapes += each(lambda n: (3, BATCHES, WIDTH, 128), f32) * 2
     shapes += each(lambda n: (3, n, 128), i16) * 2
-    shapes += each(lambda n: (3, 8, 128), f32) * 2
+    shapes += each(lambda n: (3, 1, 128), f32) * 2
     dma = pltpu.SemaphoreType.DMA
     shapes += [dma((LOADS,)), dma((3, 4, BATCHES, 2)), dma((2,)), dma((3, 2, 3, BATCHES, 2, 2)),
                dma((3, 3, BATCHES, 2, 2)), dma((3, 3, 2, 2)), dma((2, 7, 2)), dma((2, 15, 2))]
@@ -433,9 +437,9 @@
 
 def local(mantissa, scales, counts, owner_map):
     vmem, smem = pl.BlockSpec(memory_space=pltpu.VMEM), pl.BlockSpec(memory_space=pltpu.SMEM)
-    out, peak = pl.pallas_call(
+    averaged, total = pl.pallas_call(
         kernel,
-        out_shape=(jax.ShapeDtypeStruct((256, 128), jnp.bfloat16), jax.ShapeDtypeStruct((2, 128), jnp.float32)),
+        out_shape=(jax.ShapeDtypeStruct((256, 128), jnp.float32), jax.ShapeDtypeStruct((1, 128), jnp.float32)),
         in_specs=[smem, smem, pl.BlockSpec(memory_space=pl.ANY), vmem, vmem],
         out_specs=(vmem, vmem),
         scratch_shapes=scratch(),
@@ -443,6 +447,12 @@
             collective_id=0, has_side_effects=True, vmem_limit_bytes=60 * 1024 * 1024
         ),
     )(owner_map, counts, mantissa.reshape(1024, GROUP, 128), scales.reshape(256, 128), counts.reshape(1, 64))
+    out, peak = pl.pallas_call(
+        finish,
+        out_shape=(jax.ShapeDtypeStruct((256, 128), jnp.bfloat16), jax.ShapeDtypeStruct((2, 128), jnp.float32)),
+        in_specs=[vmem, vmem],
+        out_specs=(vmem, vmem),
+    )(averaged, total)
     return out, peak.reshape(256)
 
 

time: 53.7 us -> 52.2 us (0.972)
  local copies, waits for them, and re-layouts: 2.67 us -> 0 us
  Pallas kernels: 50.2 us -> 51.4 us
    unnamed x2 -> x0, local copies, waits for them, and re-layouts: 2.67 us -> none
    pallas_call x1 -> x2, Pallas kernels: 50.2 us -> 51.4 us  [the longest x1 49.6 us: local(): pl.pallas_call(kernel, out_shape=(jax.ShapeDtypeStruct((256, 128), jnp.fl...]
where the time goes in v4:
time: 52.2 us; the launch traced here: 52 us
  Pallas kernels  51.4 us (98%)
  between operations  0.64 us (1%)
    pallas_call x1, Pallas kernels, local(): pl.pallas_call(kernel, out_shape=(jax.ShapeDtypeStruct((256, 128), jnp.fl...  49.6 us
    pallas_call x1, Pallas kernels, local(): pl.pallas_call(finish, out_shape=(jax.ShapeDtypeStruct((256, 128), jnp.bf...  1.76 us

profile of v4, /device:TPU:0, one launch (start us, length us, event | category | flops | bytes accessed | tf_op | source)
XLA Modules:
  0.0 52.0 jit_solution(15005708633852715648)
XLA Ops:
  0.6 49.6 %shard_map.59 = (f32[256,128]{1,0:T(8,128)}, f32[1,128]{1,0:T(1,128)}) custom-call(s32[1024]{0:T(1024)} %owner.1, s32[64]{0:T(128)} %counts.1, bf16[1024,32,128]{2,1,0:T(8,128)(2,1)} %bitcast.4, bf16[256,128]{1,0:T(8,128)(2,1)} %bitcast.5, s32[1,64]{1,0:T(1,128)} %bitcast.6), custom_call_target="tpu_custom_call" | custom-call | tf_op jit(solution)/shard_map/pallas_call | solution.py:440
  50.3 1.8 %shard_map.60 = (bf16[256,128]{1,0:T(8,128)(2,1)}, f32[2,128]{1,0:T(2,128)}) custom-call(f32[256,128]{1,0:T(8,128)} %get-tuple-element.6.avg, f32[1,128]{1,0:T(1,128)} %get-tuple-element.7.total), custom_call_target="tpu_custom_call" | custom-call | tf_op jit(solution)/shard_map/pallas_call | solution.py:450

commit v5 on v4

--- a/solution.py
+++ b/solution.py
@@ -248,22 +248,28 @@
                 for kind in (OWN, BOTH):
                     for copy in copies1(p, d, kind, bat):
                         copy.wait_recv()
+        coded, kept = [], []
+        for p in range(3):
             for rb in ORDER:
-                h, values = rb // 2, []
+                h = rb // 2
                 for w in range(WIDTH):
                     c = bat * WIDTH + w
                     v = own[p][c * 4 + rb]
                     for d, kind in ((h, BOTH), (1 - h, OWN)):
                         v = v + restored(r1[p][d, kind, c * 2 + rb % 2], u1[p][d, kind, bat, pl.ds(w * 2 + rb % 2, 1)])
-                    values.append(v)
-                if rb:
-                    for w, v in enumerate(values):
-                        q2[p][rb - 1, bat * WIDTH + w], t2[p][rb - 1, bat, pl.ds(w, 1)] = quantize(v)
-                    for copy in copies2(p, rb, bat):
-                        copy.start()
-                else:
-                    for w, v in enumerate(values):
-                        mid[p][bat * WIDTH + w] = v
+                    if rb:
+                        coded.append((p, rb - 1, w, quantize(v)))
+                    else:
+                        kept.append((p, c, v))
+        for p, k, w, (q, step) in coded:
+            q2[p][k, bat * WIDTH + w] = q
+            t2[p][k, bat, pl.ds(w, 1)] = step
+        for p in range(3):
+            for rb in (2, 1, 3):
+                for copy in copies2(p, rb, bat):
+                    copy.start()
+        for p, c, v in kept:
+            mid[p][c] = v
 
     def copies3(p, k):
         device = peer(p, 2, k)
@@ -277,21 +283,24 @@
             for k in (1, 3, 2):
                 for copy in copies2(p, k, bat):
                     copy.wait_recv()
-            values = []
-            for w in range(WIDTH):
-                c = bat * WIDTH + w
+        for w in range(WIDTH):
+            c = bat * WIDTH + w
+            sums = []
+            for p in range(3):
                 v = mid[p][c]
                 for k in range(3):
                     v = v + restored(r2[p][k, c], u2[p][k, bat, pl.ds(w, 1)])
-                values.append(v)
-            for w, v in enumerate(values):
-                rc = ORDER[bat * WIDTH + w]
-                if rc:
-                    q3[p][rc - 1], t3[p][rc - 1] = quantize(v)
-                    for copy in copies3(p, rc):
+                sums.append(v)
+            if ORDER[c]:
+                coded = [quantize(v) for v in sums]
+                for p, (q, step) in enumerate(coded):
+                    q3[p][ORDER[c] - 1], t3[p][ORDER[c] - 1] = q, step
+                for p in range(3):
+                    for copy in copies3(p, ORDER[c]):
                         copy.start()
-                else:
-                    mid[p][3] = v
+            else:
+                for p in range(3):
+                    mid[p][c] = sums[p]
 
     def count_sources():
         for copy in count_far:
@@ -338,18 +347,21 @@
     third_dim(0)
     third_dim(1)
 
-    square = jnp.zeros((8, 128), jnp.float32)
     for p in range(3):
-        n = ROWS[p]
         for k in (1, 3, 2):
             for copy in copies3(p, k):
                 copy.wait_recv()
+    square = jnp.zeros((8, 128), jnp.float32)
+    means = []
+    for p in range(3):
         v = mid[p][3]
         for k in range(3):
             v = v + restored(r3[p][k], u3[p][k])
-        mean = v / times[pl.ds(START[p], n)]
-        avg[pl.ds(START[p], n)] = mean
-        square = square + jnp.sum((mean * mean).reshape(n // 8, 8, 128), axis=0)
+        means.append(v / times[pl.ds(START[p], ROWS[p])])
+    for mean in means:
+        square = square + jnp.sum((mean * mean).reshape(mean.shape[0] // 8, 8, 128), axis=0)
+    for p, mean in enumerate(means):
+        avg[pl.ds(START[p], ROWS[p])] = mean
 
     total = jnp.sum(square, axis=0, keepdims=True)
     red_send[0] = total

time: 52.2 us -> 51.7 us (level)
  no operation moved by 1% of the time
where the time goes in v5:
time: 51.7 us; the launch traced here: 51.5 us
  Pallas kernels  50.9 us (98%)
  between operations  0.64 us (1%)
    pallas_call x1, Pallas kernels, local(): pl.pallas_call(kernel, out_shape=(jax.ShapeDtypeStruct((256, 128), jnp.fl...  49.2 us
    pallas_call x1, Pallas kernels, local(): pl.pallas_call(finish, out_shape=(jax.ShapeDtypeStruct((256, 128), jnp.bf...  1.76 us

profile of v5, /device:TPU:0, one launch (start us, length us, event | category | flops | bytes accessed | tf_op | source)
XLA Modules:
  0.0 51.5 jit_solution(1898462889909521606)
XLA Ops:
  0.6 49.2 %shard_map.59 = (f32[256,128]{1,0:T(8,128)}, f32[1,128]{1,0:T(1,128)}) custom-call(s32[1024]{0:T(1024)} %owner.1, s32[64]{0:T(128)} %counts.1, bf16[1024,32,128]{2,1,0:T(8,128)(2,1)} %bitcast.4, bf16[256,128]{1,0:T(8,128)(2,1)} %bitcast.5, s32[1,64]{1,0:T(1,128)} %bitcast.6), custom_call_target="tpu_custom_call" | custom-call | tf_op jit(solution)/shard_map/pallas_call | solution.py:452
  49.8 1.8 %shard_map.60 = (bf16[256,128]{1,0:T(8,128)(2,1)}, f32[2,128]{1,0:T(2,128)}) custom-call(f32[256,128]{1,0:T(8,128)} %get-tuple-element.6.avg, f32[1,128]{1,0:T(1,128)} %get-tuple-element.7.total), custom_call_target="tpu_custom_call" | custom-call | tf_op jit(solution)/shard_map/pallas_call | solution.py:462
